TPU v7x, 128 devices: a whole 4x4x4 slice. The times are simulated.
128 devices in a mesh: grp: 8 (over z, y_lo), slab: 16 (over y_hi, x, core).
Axes of the slice: x: 4, y: 4 (y_hi: 2, y_lo: 2; y = y_hi * 2 + y_lo), z: 4, core: 2. Of those that a mesh axis runs over, the one named last changes fastest.
Arguments:
- orbitals: float32 [16, 96, 9216], P('grp', 'slab'), may hold values from -6 to 6
- occupation: int32 [16], P('grp'), may hold values from 1 to 4
- kernel_hat: float32 [192, 36864], P('slab'), may hold values from 0.02 to 1200, as said below
- pair_mask: int32 [1], replicated, may hold values from 1 to 7
Outputs:
- exchange_terms: float32 [16, 96, 9216], P('grp', 'slab')
Inputs may be any that keep to these rules, and one draw needn't show every extreme that they name: In this round group g is paired with group g XOR pair_mask. kernel_hat is positive, and unchanged when each frequency index k is replaced by (192 - k) mod 192 in all three dimensions at once.
All inputs are finite; a program needn't handle non-finite values.
Results may differ from a plain program's by a relative error of at most 0.0001.
Values sent between devices are 32-bit elements; how exact they have to be, the bound alone decides.
A program may use at most 64 MiB of HBM per device.

v0:
```python
import functools
import math

import jax
import jax.numpy as jnp
import ml_dtypes
import numpy as np
from jax import lax
from jax.experimental import pallas as pl
from jax.experimental.layout import Layout, with_layout_constraint
from jax.experimental.pallas import tpu as pltpu
from jax.sharding import PartitionSpec as P

MESH = pl.DeviceIdType.MESH
G = 96
N = 192
PLANES = 6
CHUNKS = 3
SLABS = 16
KZ = 12
F32 = jnp.float32
BF16 = jnp.bfloat16


def halves(table):
    table = np.asarray(table, np.float64)
    high = table.astype(np.float32).astype(ml_dtypes.bfloat16)
    low = (table - high.astype(np.float64)).astype(np.float32).astype(ml_dtypes.bfloat16)
    return np.stack([high, low])


def rotation(freq, place):
    angle = 2.0 * math.pi * ((np.outer(freq, place)) % N) / N
    return np.cos(angle), np.sin(angle)


def tables():
    every = np.arange(N)
    z = np.arange(G)
    y = np.array([4 * q + r for r in range(4) for q in range(24)])
    cos_z, sin_z = rotation(every, z)
    z_both = np.zeros((N, 256))
    z_both[:, :G], z_both[:, 128 : 128 + G] = cos_z, sin_z
    y_fwd = np.zeros((2, G, 2, 2, 128))
    for parity in range(2):
        cos_y, sin_y = rotation(2 * np.arange(G) + parity, y)
        y_fwd[0, :, 0, parity, :G] = cos_y.T
        y_fwd[1, :, 0, parity, :G] = sin_y.T
        y_fwd[0, :, 1, parity, :G] = -sin_y.T
        y_fwd[1, :, 1, parity, :G] = cos_y.T
    x_fwd, x_inv = [], []
    for c in range(CHUNKS):
        cos_x, sin_x = rotation(every, np.array([PLANES * s + 2 * c + k for k in range(2) for s in range(SLABS)]))
        pair = halves(np.block([[cos_x, sin_x], [-sin_x, cos_x]]))
        x_fwd.append(np.concatenate([pair[0], pair[0], pair[1]], axis=1))
        x_inv.append(np.concatenate([pair[0].T, pair[1].T], axis=0))
    return [halves(z_both), halves(y_fwd.reshape(N, 512)), np.stack(x_fwd), np.stack(x_inv)]


STEPS = [(1, 2), (1, 0), (0, 1), (0, 3), (1, 1), (0, 2), (1, 3)]
PEERS = [(y, x, 0) for y, x in STEPS] + [(y, x, 1) for y, x in STEPS] + [(0, 0, 1)]


def split(value):
    high = value.astype(BF16)
    return high, (value - high.astype(F32)).astype(BF16)


def dot(left, right, contract=((1,), (0,))):
    return lax.dot_general(left, right, (contract, ((), ())), preferred_element_type=F32)


def triple(left, right, contract=((1,), (0,))):
    return (
        dot(left[0], right[0], contract)
        + dot(left[0], right[1], contract)
        + dot(left[1], right[0], contract)
    )


def kernel(
    mask,
    occ_ref, orb_in, kern_in, z_in, y_in, x_in, xi_in,
    out,
    orb, kern, z_tab, y_tab, x_tab, xi_tab,
    left_copy, right, pencils, send_a, recv_a, send_b, recv_b, spec, gspec, flat, kmat,
    total, high_f, low_f, left_terms, right_terms, left_in, right_in,
    in_s, exch_s, exch_r, a_s, a_r, b_s, b_r, ret_s, ret_r,
):
    grp = lax.axis_index("grp")
    me = lax.axis_index("slab")

    def flipped(bits):
        group = grp
        for bit in range(3):
            if bits >> bit & 1:
                group = group + (1 - 2 * (grp // 2**bit % 2)) * 2**bit
        return group

    mine_y, mine_x, mine_c = me // 8, me // 2 % 4, me % 2
    peers = [((mine_y + y) % 2 * 4 + (mine_x + x) % 4) * 2 + (mine_c + c) % 2 for y, x, c in PEERS]
    crossing = mask & 1
    partner, neighbour, diagonal = flipped(mask), flipped(1), flipped(mask ^ 1)
    field_group = grp + mine_y * (neighbour - grp) if crossing else grp
    upper = field_group // 2 ** (mask.bit_length() - 1) % 2
    groups = [neighbour if crossing and y else grp for y, _, c in PEERS]
    left = left_copy if crossing else orb
    if crossing:
        gather = [(0, orb, left, 0, None), (0, orb, right, 1, partner), (1, orb, left, 0, neighbour)]
        gather.append((1, orb, right, 1, None if mask == 1 else diagonal))
        scatter = [(0, right_terms, right_in, 1, partner), (1, left_terms, left_in, 0, neighbour)]
        if mask > 1:
            scatter.append((1, right_terms, right_in, 1, diagonal))
    else:
        gather = [(None, orb, right, 1, partner)]
        scatter = [(None, right_terms, right_in, 1, partner)]

    def on_half(half, run):
        if half is None:
            run()
        else:
            pl.when(mine_y == half)(run)

    def piece(c):
        return pl.ds(864, 8) if isinstance(c, int) and c == CHUNKS else pl.ds(c * 288, 288)

    def transfer(move, sems, c):
        _, source, target, side, group = move
        s_sem, r_sem = sems
        if group is None:
            return pltpu.make_async_copy(source.at[piece(c)], target.at[piece(c)], r_sem.at[side, c])
        return pltpu.make_async_remote_copy(
            source.at[piece(c)],
            target.at[piece(c)],
            s_sem.at[side, c],
            r_sem.at[side, c],
            device_id=(group, me),
            device_id_type=MESH,
        )

    def start(moves, sems, c):
        for half in (None, 0, 1):
            chosen = [move for move in moves if move[0] == half]

            def run(chosen=chosen):
                for move in chosen:
                    transfer(move, sems, c).start()

            if chosen:
                on_half(half, run)

    def drain(moves, sems, c):
        for half in (None, 0, 1):
            chosen = [move for move in moves if move[0] == half and move[4] is not None]

            def run(chosen=chosen):
                for move in chosen:
                    transfer(move, sems, c).wait_send()

            if chosen:
                on_half(half, run)

    def arrived(moves, sems, c):
        seen = {}
        for half, _, target, side, _ in moves:
            seen.setdefault(side, (target, []))[1].append(half)
        for side, (target, halves_) in seen.items():
            def run(side=side, target=target):
                rows = piece(c)
                pltpu.make_async_copy(target.at[rows], target.at[rows], sems[1].at[side, c]).wait()

            on_half(halves_[0] if len(halves_) == 1 else None, run)

    exch, ret = (exch_s, exch_r), (ret_s, ret_r)

    barrier = pltpu.get_barrier_semaphore()
    def greet(group):
        pl.semaphore_signal(barrier, inc=1, device_id=(group, me), device_id_type=MESH)

    met = SLABS
    if crossing:
        pl.when(mine_y == 0)(lambda: greet(partner))
        pl.when(mine_y == 1)(lambda: greet(neighbour))
        if mask > 1:
            pl.when(mine_y == 1)(lambda: greet(diagonal))
            met = SLABS + mine_y
    else:
        greet(partner)
    for group, peer in zip(groups, peers):
        pl.semaphore_signal(barrier, inc=1, device_id=(group, peer), device_id_type=MESH)

    stage = [
        pltpu.make_async_copy(source, target, in_s.at[i])
        for i, (source, target) in enumerate(
            (
                (orb_in, orb.at[pl.ds(0, 864)]),
                (kern_in, kern),
                (z_in, z_tab.at[:, pl.ds(0, N), :]),
                (y_in, y_tab.at[:, pl.ds(64, N), :]),
                (x_in, x_tab),
                (xi_in, xi_tab),
            )
        )
    ]
    for copy in stage:
        copy.start()
    which = lax.broadcasted_iota(jnp.int32, (8, 128), 0)
    orb[864:872, :] = jnp.where(which == 0, occ_ref[0].astype(F32), occ_ref[1].astype(F32)) * 0.25
    pencils[...] = jnp.zeros(pencils.shape, F32)
    total[...] = jnp.zeros(total.shape, F32)
    z_tab[:, N:, :] = jnp.zeros((2, 64, 256), BF16)
    y_tab[:, :64, :] = jnp.zeros((2, 64, 512), BF16)
    y_tab[:, 64 + N :, :] = jnp.zeros((2, 64, 512), BF16)
    stage[0].wait()
    pl.semaphore_wait(barrier, met)
    for c in range(CHUNKS + 1):
        start(gather, exch, c)

    stage[1].wait()

    def flatten(step, carry):
        for sub in range(8):
            m = step * 8 + sub
            flat[pl.ds(m, KZ, stride=288), :] = kern[:, pl.ds(pl.multiple_of(m * 128, 128), 128)] * (1.0 / N**3)
        return carry

    lax.fori_loop(0, 36, flatten, 0)

    def turn(j, carry):
        pad = jnp.zeros((32, 128), F32)
        t0, t1, t2 = [
            jnp.concatenate([flat[pl.ds(j * 288 + l, G, stride=3), :], pad], axis=0).T for l in range(3)
        ]
        base = pl.multiple_of(j * N, N)
        kmat[pl.ds(base, 128), 0:128] = t0
        kmat[pl.ds(base + 128, 64), 0:128] = t1[:64]
        kmat[pl.ds(base, 64), 128:256] = t1[64:]
        kmat[pl.ds(base + 64, 128), 128:256] = t2
        return carry

    lax.fori_loop(0, KZ, turn, 0)
    for copy in stage[2:]:
        copy.wait()
    def orbital(ref, c, which):
        return [ref[pl.ds(c * 288 + 2 * l + which, 48, stride=6), :] for l in range(3)]

    def send_all(sent, landing, s_sem, r_sem, c):
        for group, peer in zip(groups, peers):
            pltpu.make_async_remote_copy(
                sent.at[pl.ds(c * 576 + peer * 36, 36)],
                landing.at[pl.ds(c * 576 + me * 36, 36)],
                s_sem.at[c],
                r_sem.at[c],
                device_id=(group, peer),
                device_id_type=MESH,
            ).start()
        rows = pl.ds(c * 576 + me * 36, 36)
        pltpu.make_async_copy(sent.at[rows], landing.at[rows], r_sem.at[c]).start()

    def wait_rows(ref, sem, start, count):
        rows = pl.ds(start, count)
        pltpu.make_async_copy(ref.at[rows], ref.at[rows], sem).wait()

    def forward_z(c, carry):
        arrived(gather, exch, c)
        first = jnp.concatenate(
            [a * b for a, b in zip(orbital(left, c, 0), orbital(right, c, upper))], axis=1
        )
        second = jnp.concatenate(
            [a * b for a, b in zip(orbital(left, c, 1), orbital(right, c, 1 - upper))], axis=1
        )
        for r in range(4):
            for k in range(2):
                one = first[24 * k : 24 * k + 24, G * r : G * r + G]
                two = second[24 * k : 24 * k + 24, G * r : G * r + G]
                at = k * N + r * 24
                pencils[at : at + 24, 0:G] = one
                pencils[at : at + 24, 128 : 128 + G] = two
                pencils[at + G : at + G + 24, 0:G] = two
                pencils[at + G : at + G + 24, 128 : 128 + G] = -one
        spread = triple((z_tab[0, :N], z_tab[1, :N]), split(pencils[...]), ((1,), (1,)))
        for l in range(3):
            send_a[pl.ds(c * 576 + l, N, stride=3), :] = spread[:, 128 * l : 128 * l + 128]
        send_all(send_a, recv_a, a_s, a_r, c)
        return carry

    lax.fori_loop(0, CHUNKS, forward_z, 0)

    def forward_y(c):
        wait_rows(recv_a, a_r.at[c], c * 576, 576)
        wire = jnp.concatenate([recv_a[pl.ds(c * 576 + l, N, stride=3), :] for l in range(3)], axis=1)
        high, low = split(wire)
        for k in range(2):
            lanes = slice(128 * k, 128 * k + 256)
            rows = slice(64, 320) if k == 0 else slice(0, 256)
            result = triple((high[:, lanes], low[:, lanes]), (y_tab[0, rows], y_tab[1, rows]))
            for l in range(4):
                spec[pl.ds(l * 384 + k * N, N), :] = result[:, 128 * l : 128 * l + 128]

    def partial_x(j, c):
        field = jnp.concatenate(
            [
                jnp.concatenate(
                    [
                        spec[pl.ds((2 * d + parity) * 384 + k * N + j, SLABS, stride=KZ), :]
                        for d in range(2)
                        for k in range(2)
                    ],
                    axis=0,
                )
                for parity in range(2)
            ],
            axis=1,
        )
        high, low = split(field)
        return dot(x_tab[c], jnp.concatenate([high, low, high], axis=0))

    def block(j):
        return pl.ds(pl.multiple_of(j * 384, 384), 384)

    def inverse_x(c, j, high, low):
        wide = dot(xi_tab[c], high)
        field = wide[:64] + wide[64:] + dot(xi_tab[c, :64], low)
        for parity in range(2):
            for d in range(2):
                for k in range(2):
                    row = (d * 2 + k) * SLABS
                    gspec[pl.ds((2 * d + parity) * 384 + k * N + j, SLABS, stride=KZ), :] = field[
                        row : row + SLABS, 128 * parity : 128 * parity + 128
                    ]

    def turn_back(j, carry):
        value = total[block(j), :] + partial_x(j, 2)
        weight = kmat[pl.ds(pl.multiple_of(j * N, N), N), :]
        high, low = split(jnp.concatenate([value[:N] * weight, value[N:] * weight], axis=0))
        high_f[block(j), :] = high
        low_f[block(j), :] = low
        inverse_x(0, j, high, low)
        return carry

    def forward(c, carry):
        forward_y(c)

        @pl.when(c < 2)
        def _():
            def add(j, carry):
                total[block(j), :] = total[block(j), :] + partial_x(j, c)
                return carry

            lax.fori_loop(0, KZ, add, 0)

        return carry

    lax.fori_loop(0, CHUNKS, forward, 0)
    lax.fori_loop(0, KZ, turn_back, 0, unroll=2)

    def inverse_y(c, carry):
        @pl.when(c > 0)
        def _():
            def back_x(j, carry):
                inverse_x(c, j, high_f[block(j), :], low_f[block(j), :])
                return carry

            lax.fori_loop(0, KZ, back_x, 0)

        parts = []
        for k in range(2):
            wide = jnp.concatenate([gspec[pl.ds(l * 384 + k * N, N), :] for l in range(4)], axis=1)
            rows = slice(64, 320) if k == 0 else slice(0, 256)
            parts.append(triple(split(wide), (y_tab[0, rows], y_tab[1, rows]), ((1,), (1,))))
        tiles = [parts[0][:, :128], parts[0][:, 128:] + parts[1][:, :128], parts[1][:, 128:]]
        for l in range(3):
            send_b[pl.ds(c * 576 + l, N, stride=3), :] = tiles[l]
        send_all(send_b, recv_b, b_s, b_r, c)
        return carry

    lax.fori_loop(0, CHUNKS, inverse_y, 0)
    arrived(gather, exch, CHUNKS)

    def inverse_z(c, carry):
        wait_rows(recv_b, b_r.at[c], c * 576, 576)
        pad = jnp.zeros((64, 128), F32)
        turned = jnp.concatenate(
            [
                jnp.concatenate([recv_b[pl.ds(c * 576 + l, N, stride=3), :], pad], axis=0).T
                for l in range(3)
            ],
            axis=0,
        )
        both = triple(split(turned), (z_tab[0], z_tab[1]))
        first, second = [], []
        for r in range(4):
            ones, twos = [], []
            for k in range(2):
                at = k * N + r * 24
                re = both[at : at + 24]
                im = both[at + G : at + G + 24]
                ones.append(re[:, :G] - im[:, 128 : 128 + G])
                twos.append(re[:, 128 : 128 + G] + im[:, :G])
            first.append(jnp.concatenate(ones, axis=0))
            second.append(jnp.concatenate(twos, axis=0))
        first = jnp.concatenate(first, axis=1)
        second = jnp.concatenate(second, axis=1)
        for field, which, other in ((first, 0, upper), (second, 1, 1 - upper)):
            near, far = orbital(left, c, which), orbital(right, c, other)
            near_w, far_w = left[pl.ds(864 + which, 1), :], right[pl.ds(864 + other, 1), :]
            for l in range(3):
                tile = field[:, 128 * l : 128 * l + 128]
                left_terms[pl.ds(c * 288 + 2 * l + which, 48, stride=6), :] = -(far_w * tile * far[l])
                right_terms[pl.ds(c * 288 + 2 * l + other, 48, stride=6), :] = -(near_w * tile * near[l])
        start(scatter, ret, c)
        return carry

    lax.fori_loop(0, CHUNKS, inverse_z, 0)

    def finish(c, carry):
        arrived(scatter, ret, c)
        rows = pl.ds(pl.multiple_of(c * 288, 288), 288)

        def lower():
            out[rows, :] = left_terms[rows, :] + right_in[rows, :]

        def higher():
            out[rows, :] = left_in[rows, :] + (right_terms if mask == 1 else right_in)[rows, :]

        if crossing:
            pl.when(mine_y == 0)(lower)
            pl.when(mine_y == 1)(higher)
        else:
            lower()
        return carry

    lax.fori_loop(0, CHUNKS, finish, 0)

    drain(gather, exch, CHUNKS)
    for c in range(CHUNKS):
        drain(gather, exch, c)
        drain(scatter, ret, c)
        wait_rows(send_a, a_s.at[c], 0, 540)
        wait_rows(send_b, b_s.at[c], 0, 540)


def local(orbitals, occupation, kernel_hat, pair_mask):
    rows = orbitals.reshape(2, PLANES, 72, 128).transpose(1, 2, 0, 3).reshape(864, 128)
    consts = [jnp.asarray(value) for value in tables()]
    dma = pltpu.SemaphoreType.DMA

    def branch(mask):
        def run(rows, occupation, kernel_hat, *consts):
            return pl.pallas_call(
                functools.partial(kernel, mask),
                out_shape=jax.ShapeDtypeStruct((864, 128), F32),
                in_specs=[pl.BlockSpec(memory_space=pltpu.SMEM)] + [pl.BlockSpec(memory_space=pl.ANY)] * 6,
                out_specs=pl.BlockSpec(memory_space=pltpu.VMEM),
                scratch_shapes=[
                    pltpu.VMEM((872, 128), F32),
                    pltpu.VMEM((KZ, N * N), F32),
                    pltpu.VMEM((2, 256, 256), BF16),
                    pltpu.VMEM((2, 320, 512), BF16),
                    pltpu.VMEM((CHUNKS, 384, N), BF16),
                    pltpu.VMEM((CHUNKS, 128, 384), BF16),
                    pltpu.VMEM((872, 128), F32),
                    pltpu.VMEM((872, 128), F32),
                    pltpu.VMEM((384, 256), F32),
                    pltpu.VMEM((1728, 128), F32),
                    pltpu.VMEM((1728, 128), F32),
                    pltpu.VMEM((1728, 128), F32),
                    pltpu.VMEM((1728, 128), F32),
                    pltpu.VMEM((1536, 128), F32),
                    pltpu.VMEM((1536, 128), F32),
                    pltpu.VMEM((KZ * 288, 128), F32),
                    pltpu.VMEM((KZ * N, 256), F32),
                    pltpu.VMEM((KZ * 384, 256), F32),
                    pltpu.VMEM((KZ * 384, 256), BF16),
                    pltpu.VMEM((KZ * 384, 256), BF16),
                    pltpu.VMEM((864, 128), F32),
                    pltpu.VMEM((864, 128), F32),
                    pltpu.VMEM((864, 128), F32),
                    pltpu.VMEM((864, 128), F32),
                    dma((6,)), dma((2, CHUNKS + 1)), dma((2, CHUNKS + 1)),
                    dma((CHUNKS,)), dma((CHUNKS,)), dma((CHUNKS,)), dma((CHUNKS,)),
                    dma((2, CHUNKS)), dma((2, CHUNKS)),
                ],
                compiler_params=pltpu.CompilerParams(
                    collective_id=mask, has_side_effects=True, vmem_limit_bytes=56 * 2**20
                ),
                name=f"exchange_{mask}",
            )(occupation, rows, kernel_hat, *consts)

        return run

    result = lax.switch(
        pair_mask[0] - 1, [branch(mask) for mask in range(1, 8)], rows, occupation, kernel_hat, *consts
    )
    planes = result.reshape(PLANES, 72, 2, 128).transpose(2, 0, 1, 3)
    planes = with_layout_constraint(planes, Layout((1, 2, 0, 3)))
    return planes.reshape(2, PLANES, G * G)


def solution(mesh):
    return jax.shard_map(
        local,
        mesh=mesh,
        in_specs=(P("grp", "slab", None), P("grp"), P("slab", None), P()),
        out_specs=P("grp", "slab", None),
        check_vma=False,
    )
```

profile of v0, /device:TPU:1, one launch (start us, length us, event | category | flops | bytes accessed | tf_op | source)
XLA Modules:
  0.0 50.8 jit_solution(230339104291322871)
XLA Ops:
  0.7 49.3 %conditional.1 = (f32[864,128]{1,0:T(8,128)S(1)}) conditional(s32[]{:T(128)} %bitcast, (s32[2]{0:T(128)}, f32[864,128]{1,0:T(8,128)}, f32[12,36864]{1,0:T(8,128)}, bf16[2,192,256]{2,1,0:T(8,128)(2,1)}, bf16[2,192,512]{2,1,0:T(8,128)(2,1)}, /*index=5*/bf16[3,384,192]{2,1,0:T(8,128)(2,1)}, ...), branch_computations={%region_0.0_spmd, %region_1.0_spmd, %region_2.0_spmd, %region_3.0_... | conditional | bytes 8 | solution.py:492
  0.7 49.1 %exchange_3.1 = f32[864,128]{1,0:T(8,128)S(1)} custom-call(s32[2]{0:T(128)} %get-tuple-element.125.occ_ref, f32[864,128]{1,0:T(8,128)} %get-tuple-element.126.orb_in, f32[12,36864]{1,0:T(8,128)} %get-tuple-element.127.kern_in, bf16[2,192,256]{2,1,0:T(8,128)(2,1)} %get-tuple-element.128.z_in, bf16[2,192,512]{2,1,0:T(8,128)(2,1)} %get-tuple-element.129.y_in, ...), custom_call_target="tpu_custom_call" | custom-call | tf_op jit(solution)/shard_map/cond/branch_2_fun/exchange_3/pallas_call | solution.py:450
  50.0 0.8 %copy.19 = f32[2,6,9216]{2,0,1:T(2,128)} copy(f32[2,6,9216]{2,0,1:T(2,128)S(1)} %bitcast.18) | data formatting | bytes 884736
where the time goes:
time: 50.8 us
  Pallas kernels  49.1 us (97%)
  local copies, waits for them, and re-layouts  0.76 us (1%)
  between operations  0.66 us (1%)
    pallas_call x1, Pallas kernels, run(): pl.pallas_call(functools.partial(kernel, mask), out_shape=jax.ShapeDtypeS...  49.1 us

commit v1 on v0

--- a/solution.py
+++ b/solution.py
@@ -207,7 +207,12 @@
     which = lax.broadcasted_iota(jnp.int32, (8, 128), 0)
     orb[864:872, :] = jnp.where(which == 0, occ_ref[0].astype(F32), occ_ref[1].astype(F32)) * 0.25
     pencils[...] = jnp.zeros(pencils.shape, F32)
-    total[...] = jnp.zeros(total.shape, F32)
+
+    def clear(step, carry):
+        total[pl.ds(pl.multiple_of(step * 96, 96), 96), :] = jnp.zeros((96, 256), F32)
+        return carry
+
+    lax.fori_loop(0, 48, clear, 0)
     z_tab[:, N:, :] = jnp.zeros((2, 64, 256), BF16)
     y_tab[:, :64, :] = jnp.zeros((2, 64, 512), BF16)
     y_tab[:, 64 + N :, :] = jnp.zeros((2, 64, 512), BF16)
@@ -352,7 +357,7 @@
         return carry
 
     lax.fori_loop(0, CHUNKS, forward, 0)
-    lax.fori_loop(0, KZ, turn_back, 0, unroll=2)
+    lax.fori_loop(0, KZ, turn_back, 0, unroll=6)
 
     def inverse_y(c, carry):
         @pl.when(c > 0)

time: 50.8 us -> 53.4 us (1.051)
  Pallas kernels: 49.1 us -> 51.1 us
    pallas_call x1, Pallas kernels: 49.1 us -> 51.1 us  [run(): pl.pallas_call(functools.partial(kernel, mask), out_shape=jax.ShapeDtypeS...]
where the time goes in v1:
time: 53.4 us; the launch traced here: 53.1 us
  Pallas kernels  51.1 us (96%)
  local copies, waits for them, and re-layouts  0.76 us (1%)
  between operations  0.66 us (1%)
    pallas_call x1, Pallas kernels, run(): pl.pallas_call(functools.partial(kernel, mask), out_shape=jax.ShapeDtypeS...  51.1 us

profile of v1, /device:TPU:1, one launch (start us, length us, event | category | flops | bytes accessed | tf_op | source)
XLA Modules:
  0.0 53.1 jit_solution(10067830912615726447)
XLA Ops:
  0.7 51.6 %conditional.1 = (f32[864,128]{1,0:T(8,128)S(1)}) conditional(s32[]{:T(128)} %bitcast, (s32[2]{0:T(128)}, f32[864,128]{1,0:T(8,128)}, f32[12,36864]{1,0:T(8,128)}, bf16[2,192,256]{2,1,0:T(8,128)(2,1)}, bf16[2,192,512]{2,1,0:T(8,128)(2,1)}, /*index=5*/bf16[3,384,192]{2,1,0:T(8,128)(2,1)}, ...), branch_computations={%region_0.0_spmd, %region_1.0_spmd, %region_2.0_spmd, %region_3.0_... | conditional | bytes 8 | solution.py:497
  0.9 51.1 %exchange_6.1 = f32[864,128]{1,0:T(8,128)S(1)} custom-call(s32[2]{0:T(128)} %get-tuple-element.146.occ_ref, f32[864,128]{1,0:T(8,128)} %get-tuple-element.147.orb_in, f32[12,36864]{1,0:T(8,128)} %get-tuple-element.148.kern_in, bf16[2,192,256]{2,1,0:T(8,128)(2,1)} %get-tuple-element.149.z_in, bf16[2,192,512]{2,1,0:T(8,128)(2,1)} %get-tuple-element.150.y_in, ...), custom_call_target="tpu_custom_call" | custom-call | tf_op jit(solution)/shard_map/cond/branch_5_fun/exchange_6/pallas_call | solution.py:455
  52.3 0.8 %copy.19 = f32[2,6,9216]{2,0,1:T(2,128)} copy(f32[2,6,9216]{2,0,1:T(2,128)S(1)} %bitcast.18) | data formatting | bytes 884736
